TPU v7x, 32 devices: a whole 2x2x4 slice. The times are simulated.
32 devices in a mesh: frag: 2 (over x), grid: 16 (over z, y, core).
Axes of the slice: x: 2, y: 2, z: 4, core: 2. Of those that a mesh axis runs over, the one named last changes fastest.
Arguments:
- psi: float32 [16384, 640], P(('frag', 'grid')), parts along dimension 0
- order: int32 [10], P('frag'), parts along dimension 0, may hold values from 0 to 4, each once
Outputs:
- orthonormal: float32 [16384, 640], P(('frag', 'grid')), parts along dimension 0
There are 2 independent parts, one for each index of `frag`. A program takes and returns all parts, laid end to end along the dimension named above; each array names one. Nothing has to cross between parts.
All inputs are finite; a program needn't handle non-finite values.
Results may differ from a plain program's by a relative error of at most 0.00012.
Values sent between devices are 32-bit elements; how exact they have to be, the bound alone decides.
A program may use at most 64 MiB of HBM per device.

v0:
```python
import functools

import jax
import jax.numpy as jnp
from jax import lax
from jax.experimental import pallas as pl
from jax.experimental.pallas import tpu as pltpu
from jax.sharding import PartitionSpec as P

BLOCK = 128
PANEL = 16
TILE = 8
HIGHEST = lax.Precision.HIGHEST


def dot(left, right, dims):
    return lax.dot_general(
        left, right, (dims, ((), ())), precision=HIGHEST, preferred_element_type=jnp.float32
    )


def pairs(count):
    return [(i, j) for i in range(count) for j in range(i, count)]


def slot(i, j, count):
    return i * count - (i * (i - 1)) // 2 + (j - i)


def piece_ends(count, devices):
    unit, total, ends = devices * TILE, 0, [0]
    for i in range(count):
        total += (count - i) * BLOCK
        end = -(-total // unit) * unit
        if i != count - 2 and end > ends[-1]:
            ends.append(end)
    return ends


def gram_kernel(bits, scale, ends, psi_ref, out_ref, part, acc, recv, full, send_sem, recv_sem):
    me = lax.axis_index("grid")
    digit = [(me // 2**k) % 2 for k in range(bits)]
    partners = [me + (1 - 2 * digit[k]) * 2**k for k in range(bits)]
    rows = part.shape[0]
    count = psi_ref.shape[1] // BLOCK
    pieces = len(ends) - 1
    turn = 1 + (bits - 1) // 2
    routes = [
        list(range(bits)) if p % 2 == 0 else [0, *range(turn, bits), *range(1, turn)]
        for p in range(pieces)
    ]
    offset = ends[:-1]
    size = [ends[p + 1] - ends[p] for p in range(pieces)]
    base = ends[:-1]
    copies = [None] * pieces

    barrier = pltpu.get_barrier_semaphore()
    for partner in partners:
        pl.semaphore_signal(
            barrier, inc=1, device_id={"grid": partner}, device_id_type=pl.DeviceIdType.MESH
        )

    def send(p, src, dst, step, k):
        copies[p] = pltpu.make_async_remote_copy(
            src_ref=src,
            dst_ref=dst,
            send_sem=send_sem.at[p, step],
            recv_sem=recv_sem.at[p, step],
            device_id={"grid": partners[k]},
            device_id_type=pl.DeviceIdType.MESH,
        )
        copies[p].start()

    def scatter(p, step):
        k = routes[p][step]
        half = size[p] // 2
        give = pl.multiple_of(offset[p] + (1 - digit[k]) * half, TILE)
        source = part if step == 0 else acc
        send(p, source.at[pl.ds(give, half)], recv.at[pl.ds(base[p], half)], step, k)

    def reduce(p, step):
        k = routes[p][step]
        half = size[p] // 2
        keep = pl.multiple_of(offset[p] + digit[k] * half, TILE)
        copies[p].wait()
        source = part if step == 0 else acc
        target = full if step == bits - 1 else acc
        target[pl.ds(keep, half), :] = source[pl.ds(keep, half), :] + recv[base[p] : base[p] + half, :]
        offset[p], size[p], base[p] = keep, half, base[p] + half

    def gather(p, step):
        here = full.at[pl.ds(pl.multiple_of(offset[p], TILE), size[p])]
        send(p, here, here, bits + step, routes[p][step])

    def widen(p, step):
        copies[p].wait()
        offset[p] = offset[p] - digit[routes[p][step]] * size[p]
        size[p] *= 2

    at, begun = 0, 0
    for i in range(count):
        left = psi_ref[:, i * BLOCK : (i + 1) * BLOCK]
        row = dot(left, psi_ref[:, i * BLOCK :], ((0,), (0,))) * scale
        for j in range(i, count):
            part[at : at + BLOCK, :] = row[:, (j - i) * BLOCK : (j - i + 1) * BLOCK]
            at += BLOCK
        if i == count - 1 and at < rows:
            part[at:, :] = jnp.zeros((rows - at, BLOCK), jnp.float32)
            at = rows
        if i == 0:
            pl.semaphore_wait(barrier, bits)
        while begun < pieces and ends[begun + 1] <= at:
            scatter(begun, 0)
            begun += 1

    for step in range(bits):
        for p in range(pieces):
            reduce(p, step)
            if step < bits - 1:
                scatter(p, step + 1)
            else:
                gather(p, step)
    for step in reversed(range(bits)):
        for p in range(pieces):
            widen(p, step)
            if step > 0:
                gather(p, step - 1)
    out_ref[...] = full[: out_ref.shape[0], :]


def packed_gram(psi, devices):
    points, bands = psi.shape
    count = bands // BLOCK
    used = len(pairs(count)) * BLOCK
    ends = piece_ends(count, devices)
    bits = devices.bit_length() - 1
    scale = float(1.0 / (points * devices))
    buffer = pltpu.VMEM((ends[-1], BLOCK), jnp.float32)
    semaphores = pltpu.SemaphoreType.DMA((len(ends) - 1, 2 * bits))
    return pl.pallas_call(
        functools.partial(gram_kernel, bits, scale, ends),
        out_shape=jax.ShapeDtypeStruct((used, BLOCK), jnp.float32),
        in_specs=[pl.BlockSpec(memory_space=pltpu.VMEM)],
        out_specs=pl.BlockSpec(memory_space=pltpu.VMEM),
        scratch_shapes=[buffer, buffer, buffer, buffer, semaphores, semaphores],
        compiler_params=pltpu.CompilerParams(collective_id=0, has_side_effects=True),
    )(psi)


def thirds(value):
    high = value.astype(jnp.bfloat16)
    value = value - high.astype(jnp.float32)
    middle = value.astype(jnp.bfloat16)
    return high, middle, (value - middle.astype(jnp.float32)).astype(jnp.bfloat16)


def factor_block(gram):
    tiles = PANEL // TILE
    row = lax.broadcasted_iota(jnp.int32, (TILE, BLOCK), 0)
    lane = lax.broadcasted_iota(jnp.int32, (TILE, BLOCK), 1)
    rest, done = gram, []
    for start in range(0, BLOCK, PANEL):
        panel = [rest[r * TILE : (r + 1) * TILE, :] for r in range(tiles)]
        columns = [
            [jnp.broadcast_to(panel[r][:, start + j : start + j + 1], (TILE, BLOCK)) for r in range(tiles)]
            for j in range(PANEL)
        ]
        inside = (lane >= start) & (lane < start + PANEL)
        panel = [
            jnp.where(inside, jnp.where(lane == row + (start + r * TILE), 1.0, 0.0), panel[r])
            for r in range(tiles)
        ]
        pivots = [jnp.ones((TILE, BLOCK), jnp.float32)] * tiles
        for j in range(PANEL):
            own, sub = divmod(j, TILE)
            pivot = jnp.broadcast_to(columns[j][own][sub : sub + 1, :], (TILE, BLOCK))
            pivots[own] = jnp.where(row == sub, pivot, pivots[own])
            if j == PANEL - 1:
                break
            inverse = 1.0 / pivot
            factors = {}
            for r in range(own, tiles):
                value = columns[j][r] * inverse
                factors[r] = jnp.where(row > sub, value, 0.0) if r == own else value
            targets = columns[j + 1 :] + [panel]
            for target in targets:
                top = jnp.broadcast_to(target[own][sub : sub + 1, :], (TILE, BLOCK))
                for r in range(own, tiles):
                    target[r] = target[r] - factors[r] * top
        norm = jnp.concatenate([panel[r] * lax.rsqrt(pivots[r]) for r in range(tiles)], axis=0)
        wide = lax.broadcasted_iota(jnp.int32, (PANEL, BLOCK), 1)
        done.append(jnp.where(wide < start + PANEL, norm, 0.0))
        left = BLOCK - start - PANEL
        if left:
            high, middle, low = thirds(norm)
            left_parts = jnp.concatenate([low, high, middle, middle, high, high], axis=0)
            right_parts = jnp.concatenate([high, low, middle, high, middle, high], axis=0)
            turned = left_parts.T
            cuts = [start + PANEL, start + 2 * PANEL, BLOCK]
            update = jnp.concatenate(
                [
                    jnp.dot(turned[a:b, :], right_parts, preferred_element_type=jnp.float32)
                    for a, b in zip(cuts, cuts[1:])
                    if a < b
                ],
                axis=0,
            )
            wide = lax.broadcasted_iota(jnp.int32, (left, BLOCK), 1)
            inside = (wide >= start) & (wide < start + PANEL)
            rest = jnp.where(inside, 0.0, rest[PANEL:, :]) - update
    return jnp.concatenate(done, axis=0)


def factor_kernel(count, order_ref, packed_ref, psi_ref, out_ref, work, x):
    def piece(s, t):
        a, b = order_ref[s], order_ref[t]
        low, high = jnp.minimum(a, b), jnp.maximum(a, b)
        at = pl.multiple_of(slot(low, high, count) * BLOCK, BLOCK)
        value = packed_ref[pl.ds(at, BLOCK), :]
        return jnp.where(a <= b, value, value.T)

    def span(i):
        return slice(i * BLOCK, (i + 1) * BLOCK)

    def home(s):
        return pl.ds(pl.multiple_of(order_ref[s] * BLOCK, BLOCK), BLOCK)

    for s, t in pairs(count):
        work[span(s), span(t)] = piece(s, t)
    for s in range(count):
        x[:, span(s)] = psi_ref[:, home(s)]

    for s in range(count):
        inverse = factor_block(work[span(s), span(s)])
        if s < count - 1:
            after = (s + 1) * BLOCK
            norm = dot(inverse, work[span(s), after:], ((1,), (0,)))
            for r in range(s + 1, count):
                skip = r * BLOCK - after
                left = norm[:, skip : skip + BLOCK]
                work[span(r), r * BLOCK :] -= dot(left, norm[:, skip:], ((0,), (0,)))
        q = dot(x[:, span(s)], inverse, ((1,), (1,)))
        out_ref[:, home(s)] = q
        if s < count - 1:
            x[:, after:] -= dot(q, norm, ((1,), (0,)))


def orthonormalize(packed, psi, order):
    count = order.shape[0]
    rows, bands = psi.shape
    vmem = pl.BlockSpec(memory_space=pltpu.VMEM)
    return pl.pallas_call(
        functools.partial(factor_kernel, count),
        out_shape=jax.ShapeDtypeStruct((rows, bands), jnp.float32),
        in_specs=[pl.BlockSpec(memory_space=pltpu.SMEM), vmem, vmem],
        out_specs=vmem,
        scratch_shapes=[
            pltpu.VMEM((bands, bands), jnp.float32),
            pltpu.VMEM((rows, bands), jnp.float32),
        ],
    )(order, packed, psi)


def solution(mesh):
    devices = mesh.shape["grid"]

    def local(psi, order):
        return orthonormalize(packed_gram(psi, devices), psi, order)

    in_specs = (P(("frag", "grid"), None), P("frag"))
    out_specs = P(("frag", "grid"), None)
    return jax.shard_map(local, mesh=mesh, in_specs=in_specs, out_specs=out_specs, check_vma=False)
```

profile of v0, /device:TPU:0, one launch (start us, length us, event | category | flops | bytes accessed | tf_op | source)
XLA Modules:
  0.0 58.3 jit_solution(14881465838904320498)
XLA Ops:
  0.0 33.1 %shard_map.28.packed_ref = f32[1920,128]{1,0:T(8,128)} custom-call(f32[512,640]{1,0:T(8,128)} %psi_ref.3), custom_call_target="tpu_custom_call" | custom-call | tf_op jit(solution)/shard_map/pallas_call | solution.py:140
  33.1 25.2 %shard_map.29 = f32[512,640]{1,0:T(8,128)} custom-call(s32[5]{0:T(128)} %order_ref.1, f32[1920,128]{1,0:T(8,128)} %shard_map.28.packed_ref, f32[512,640]{1,0:T(8,128)} %psi_ref.3), custom_call_target="tpu_custom_call" | custom-call | tf_op jit(solution)/shard_map/pallas_call | solution.py:252
where the time goes:
time: 58.5 us; the launch traced here: 58.3 us
  Pallas kernels  58.3 us (100%)
    pallas_call x1, Pallas kernels, packed_gram(): pl.pallas_call(functools.partial(gram_kernel, bits, scale, ends), out_sha...  33.1 us
    pallas_call x1, Pallas kernels, orthonormalize(): pl.pallas_call(functools.partial(factor_kernel, count), out_shape=jax.Sha...  25.2 us

commit v1 on v0

v1 whole, which is shorter than its diff:
```python
import functools

import jax
import jax.numpy as jnp
from jax import lax
from jax.experimental import pallas as pl
from jax.experimental.pallas import tpu as pltpu
from jax.sharding import PartitionSpec as P

BLOCK = 128
PANEL = 16
TILE = 8
HIGHEST = lax.Precision.HIGHEST


def dot(left, right, dims):
    return lax.dot_general(
        left, right, (dims, ((), ())), precision=HIGHEST, preferred_element_type=jnp.float32
    )


CUTS = ((), (1,), (1,), (1, 2), (1, 2))
EVENTS = (
    (1, 2, 0, 3, 4, 1, 0),
    (2, 3), (4,), (1,), (2,), (3,), (1, 4), (2,), (3,),
    (4,), (3,), (4,), (3,), (4,), (4,),
)


def thirds(value):
    high = value.astype(jnp.bfloat16)
    value = value - high.astype(jnp.float32)
    middle = value.astype(jnp.bfloat16)
    return high, middle, (value - middle.astype(jnp.float32)).astype(jnp.bfloat16)


def factor_block(gram, result):
    tiles = PANEL // TILE
    row = lax.broadcasted_iota(jnp.int32, (TILE, BLOCK), 0)
    lane = lax.broadcasted_iota(jnp.int32, (TILE, BLOCK), 1)
    rest, done = gram, []
    for start in range(0, BLOCK, PANEL):
        panel = [rest[r * TILE : (r + 1) * TILE, :] for r in range(tiles)]
        columns = [
            [jnp.broadcast_to(panel[r][:, start + j : start + j + 1], (TILE, BLOCK)) for r in range(tiles)]
            for j in range(PANEL)
        ]
        inside = (lane >= start) & (lane < start + PANEL)
        panel = [
            jnp.where(inside, jnp.where(lane == row + (start + r * TILE), 1.0, 0.0), panel[r])
            for r in range(tiles)
        ]
        pivots = [jnp.ones((TILE, BLOCK), jnp.float32)] * tiles
        for j in range(PANEL):
            own, sub = divmod(j, TILE)
            pivot = jnp.broadcast_to(columns[j][own][sub : sub + 1, :], (TILE, BLOCK))
            pivots[own] = jnp.where(row == sub, pivot, pivots[own])
            if j == PANEL - 1:
                break
            inverse = 1.0 / pivot
            factors = {}
            for r in range(own, tiles):
                value = columns[j][r] * inverse
                factors[r] = jnp.where(row > sub, value, 0.0) if r == own else value
            targets = columns[j + 1 :] + [panel]
            for target in targets:
                top = jnp.broadcast_to(target[own][sub : sub + 1, :], (TILE, BLOCK))
                for r in range(own, tiles):
                    target[r] = target[r] - factors[r] * top
        norm = jnp.concatenate([panel[r] * lax.rsqrt(pivots[r]) for r in range(tiles)], axis=0)
        wide = lax.broadcasted_iota(jnp.int32, (PANEL, BLOCK), 1)
        done.append(jnp.where(wide < start + PANEL, norm, 0.0))
        yield
        left = BLOCK - start - PANEL
        if left:
            high, middle, low = thirds(norm)
            left_parts = jnp.concatenate([low, high, middle, middle, high, high], axis=0)
            right_parts = jnp.concatenate([high, low, middle, high, middle, high], axis=0)
            turned = left_parts.T
            cuts = [start + PANEL, start + 2 * PANEL, BLOCK]
            update = jnp.concatenate(
                [
                    jnp.dot(turned[a:b, :], right_parts, preferred_element_type=jnp.float32)
                    for a, b in zip(cuts, cuts[1:])
                    if a < b
                ],
                axis=0,
            )
            wide = lax.broadcasted_iota(jnp.int32, (left, BLOCK), 1)
            inside = (wide >= start) & (wide < start + PANEL)
            rest = jnp.where(inside, 0.0, rest[PANEL:, :]) - update
    result.append(jnp.concatenate(done, axis=0))


class Exchange:
    def __init__(self, bits, refs):
        self.me = lax.axis_index("grid")
        self.digit = [(self.me // 2**k) % 2 for k in range(bits)]
        self.part, self.acc, self.recv, self.full, self.send_sem, self.recv_sem = refs
        self.used = 0
        self.sent = []

    def toward(self, low, delta):
        shift = 0
        for k in range(delta.bit_length()):
            if (delta >> k) & 1:
                shift = shift + (1 - 2 * self.digit[low + k]) * 2**k
        return shift

    def send(self, src, dst, low, delta):
        copy = pltpu.make_async_remote_copy(
            src_ref=src,
            dst_ref=dst,
            send_sem=self.send_sem.at[self.used],
            recv_sem=self.recv_sem.at[self.used],
            device_id={"grid": self.me + self.toward(low, delta) * 2**low},
            device_id_type=pl.DeviceIdType.MESH,
        )
        copy.start()
        self.used += 1
        self.sent.append(copy)
        return copy

    def steps(self, at, rows, stages):
        offset, size, base = at, rows, at
        last = len(stages) - 1
        for i, (low, high) in enumerate(stages):
            group = 2 ** (high - low)
            own = (self.me // 2**low) % group
            sub = size // group
            source = self.part if i == 0 else self.acc
            copies = []
            for delta in range(1, group):
                give = pl.multiple_of(offset + (own + self.toward(low, delta)) * sub, TILE)
                slot = base + (delta - 1) * sub
                copies.append(
                    self.send(source.at[pl.ds(give, sub)], self.recv.at[pl.ds(slot, sub)], low, delta)
                )
            yield
            keep = pl.multiple_of(offset + own * sub, TILE)
            total = source[pl.ds(keep, sub), :]
            for delta, copy in enumerate(copies):
                copy.wait_recv()
                total = total + self.recv[base + delta * sub : base + (delta + 1) * sub, :]
            target = self.full if i == last else self.acc
            target[pl.ds(keep, sub), :] = total
            offset, size, base = keep, sub, base + (group - 1) * sub
        for low, high in reversed(stages):
            group = 2 ** (high - low)
            own = (self.me // 2**low) % group
            here = self.full.at[pl.ds(pl.multiple_of(offset, TILE), size)]
            copies = [self.send(here, here, low, delta) for delta in range(1, group)]
            yield
            for copy in copies:
                copy.wait_recv()
            offset, size = offset - own * size, size * group


def stages_of(bits, column):
    cuts = sorted({0, *CUTS[min(column, len(CUTS) - 1)], bits})
    cuts = [c for c in cuts if c <= bits]
    return list(zip(cuts, cuts[1:]))


def copies_of(stages):
    return 2 * sum(2 ** (high - low) - 1 for low, high in stages)


def fused_kernel(
    bits, scale, ats, order_ref, psi_ref, q,
    x, part, acc, recv, full, work, norms, inverses, send_sem, recv_sem,
):
    count = order_ref.shape[0]
    me = lax.axis_index("grid")

    def span(i):
        return slice(i * BLOCK, (i + 1) * BLOCK)

    barrier = pltpu.get_barrier_semaphore()
    exchange = Exchange(bits, (part, acc, recv, full, send_sem, recv_sem))
    for delta in range(1, 2**bits):
        pl.semaphore_signal(
            barrier,
            inc=1,
            device_id={"grid": me + exchange.toward(0, delta)},
            device_id_type=pl.DeviceIdType.MESH,
        )

    for s in range(count):
        which = jnp.full((psi_ref.shape[0], BLOCK), order_ref[s], jnp.int32)
        block = psi_ref[:, span(0)]
        for b in range(1, count):
            block = jnp.where(which == b, psi_ref[:, span(b)], block)
        x[:, span(s)] = block

    pieces = []
    for t in range(count):
        at, rows = ats[t], (t + 1) * BLOCK
        part[at : at + rows, :] = dot(x[:, :rows], x[:, span(t)], ((0,), (0,))) * scale
        if at + rows < ats[t + 1]:
            part[at + rows : ats[t + 1], :] = jnp.zeros((ats[t + 1] - at - rows, BLOCK), jnp.float32)
        if t == 0:
            pl.semaphore_wait(barrier, 2**bits - 1)
        pieces.append(exchange.steps(at, ats[t + 1] - at, stages_of(bits, t)))
        next(pieces[t])

    alive = [True] * count

    def advance(t):
        if alive[t] and next(pieces[t], None) is None and pieces[t].gi_frame is None:
            alive[t] = False
            for r in range(t + 1):
                work[span(r), span(t)] = full[ats[t] + r * BLOCK : ats[t] + (r + 1) * BLOCK, :]

    def apply(s, t):
        norm = dot(inverses[span(s), :], work[span(s), span(t)], ((1,), (0,)))
        norms[span(s), span(t)] = norm
        left = norms[span(s), (s + 1) * BLOCK : (t + 1) * BLOCK]
        work[(s + 1) * BLOCK : (t + 1) * BLOCK, span(t)] -= dot(left, norm, ((0,), (0,)))

    def project(s, t):
        x[:, span(t)] -= dot(q[:, span(s)], norms[span(s), span(t)], ((1,), (0,)))

    todo = []
    events = list(EVENTS)
    for t in events.pop(0):
        advance(t)
    while alive[0]:
        advance(0)
    for s in range(count):
        while alive[s]:
            advance(s)
        for u in range(s):
            if ("a", u, s) in todo:
                todo.remove(("a", u, s))
                apply(u, s)
        result = []
        for _ in factor_block(work[span(s), span(s)], result):
            for t in events.pop(0) if events else ():
                if t < count:
                    advance(t)
            for item in [i for i in todo if i[0] == "a" and not alive[i[2]]][:1]:
                todo.remove(item)
                apply(item[1], item[2])
            else:
                for item in [i for i in todo if i[0] == "x" and ("a", i[1], i[2]) not in todo][:1]:
                    todo.remove(item)
                    project(item[1], item[2])
        inverses[span(s), :] = result[0]
        todo += [("a", s, t) for t in range(s + 1, count)]
        for u in range(s):
            if ("x", u, s) in todo:
                todo.remove(("x", u, s))
                project(u, s)
        q[:, span(s)] = dot(x[:, span(s)], inverses[span(s), :], ((1,), (1,)))
        todo += [("x", s, t) for t in range(s + 1, count)]

    for copy in exchange.sent:
        copy.wait_send()


def orthonormalize(devices, psi, order):
    count = order.shape[0]
    points, bands = psi.shape
    bits = devices.bit_length() - 1
    unit, ats = devices * TILE, [0]
    for t in range(count):
        ats.append(ats[-1] + -(-(t + 1) * BLOCK // unit) * unit)
    copies = sum(copies_of(stages_of(bits, t)) for t in range(count))
    scale = float(1.0 / (points * devices))
    vmem = pl.BlockSpec(memory_space=pltpu.VMEM)
    buffer = pltpu.VMEM((ats[-1], BLOCK), jnp.float32)
    square = pltpu.VMEM((bands, bands), jnp.float32)
    tall = pltpu.VMEM((points, bands), jnp.float32)
    semaphores = pltpu.SemaphoreType.DMA((copies,))
    return pl.pallas_call(
        functools.partial(fused_kernel, bits, scale, ats),
        out_shape=jax.ShapeDtypeStruct((points, bands), jnp.float32),
        in_specs=[pl.BlockSpec(memory_space=pltpu.SMEM), vmem],
        out_specs=vmem,
        scratch_shapes=[
            tall, buffer, buffer, buffer, buffer, square, square,
            pltpu.VMEM((bands, BLOCK), jnp.float32), semaphores, semaphores,
        ],
        compiler_params=pltpu.CompilerParams(collective_id=0, has_side_effects=True),
    )(order, psi)


def place_kernel(order_ref, q_ref, out_ref, held, in_sem, out_sem):
    count = order_ref.shape[0]
    loads, stores = [], []
    for s in range(count):
        columns = slice(s * BLOCK, (s + 1) * BLOCK)
        loads.append(pltpu.make_async_copy(q_ref.at[:, columns], held.at[s], in_sem.at[s]))
        loads[s].start()
    for s in range(count):
        home = pl.ds(pl.multiple_of(order_ref[s] * BLOCK, BLOCK), BLOCK)
        stores.append(pltpu.make_async_copy(held.at[s], out_ref.at[:, home], out_sem.at[s]))
        loads[s].wait()
        stores[s].start()
    for s in range(count):
        stores[s].wait()


def place(q, order):
    count = order.shape[0]
    rows, bands = q.shape
    anywhere = pl.BlockSpec(memory_space=pl.ANY)
    semaphores = pltpu.SemaphoreType.DMA((count,))
    return pl.pallas_call(
        place_kernel,
        out_shape=jax.ShapeDtypeStruct((rows, bands), jnp.float32),
        in_specs=[pl.BlockSpec(memory_space=pltpu.SMEM), anywhere],
        out_specs=anywhere,
        scratch_shapes=[pltpu.VMEM((count, rows, BLOCK), jnp.float32), semaphores, semaphores],
    )(order, q)


def solution(mesh):
    devices = mesh.shape["grid"]

    def local(psi, order):
        return place(orthonormalize(devices, psi, order), order)

    in_specs = (P(("frag", "grid"), None), P("frag"))
    out_specs = P(("frag", "grid"), None)
    return jax.shard_map(local, mesh=mesh, in_specs=in_specs, out_specs=out_specs, check_vma=False)
```

time: 58.5 us -> 57.2 us (0.978)
  Pallas kernels: 58.3 us -> 56.9 us
    pallas_call x2, Pallas kernels: 58.3 us -> 56.9 us  [the longest x1 54.1 us: orthonormalize(): pl.pallas_call(functools.partial(fused_kernel, bits, scale, ats), out_sha...]
where the time goes in v1:
time: 57.2 us; the launch traced here: 57 us
  Pallas kernels  56.9 us (99%)
    pallas_call x1, Pallas kernels, orthonormalize(): pl.pallas_call(functools.partial(fused_kernel, bits, scale, ats), out_sha...  54.1 us
    pallas_call x1, Pallas kernels, place(): pl.pallas_call(place_kernel, out_shape=jax.ShapeDtypeStruct((rows, bands)...  2.75 us

profile of v1, /device:TPU:0, one launch (start us, length us, event | category | flops | bytes accessed | tf_op | source)
XLA Modules:
  0.0 57.0 jit_solution(3347713807947165941)
XLA Ops:
  0.0 54.1 %shard_map.28.q_ref = f32[512,640]{1,0:T(8,128)} custom-call(s32[5]{0:T(128)} %order_ref.3, f32[512,640]{1,0:T(8,128)} %psi_ref.1), custom_call_target="tpu_custom_call" | custom-call | tf_op jit(solution)/shard_map/pallas_call | solution.py:276
  54.1 2.7 %shard_map.29 = f32[512,640]{1,0:T(8,128)} custom-call(s32[5]{0:T(128)} %order_ref.3, f32[512,640]{1,0:T(8,128)} %shard_map.28.q_ref), custom_call_target="tpu_custom_call" | custom-call | tf_op jit(solution)/shard_map/pallas_call | solution.py:310
